TPU v7x, 32 devices: a whole 2x2x4 slice. The times are simulated.
32 devices in a mesh: ta: 16 (over z, y, x), gz: 2 (over core).
Axes of the slice: x: 2, y: 2, z: 4, core: 2. Of those that a mesh axis runs over, the one named last changes fastest.
Arguments:
- propagator: float32 [2, 12, 12, 16, 13824], P(None, None, None, 'ta', 'gz'), may hold values from -6 to 6
- backward: float32 [2, 12, 12, 16, 13824], P(None, None, None, 'ta', 'gz'), may hold values from -6 to 6
- sink_time: int32 [1], replicated, may hold values from 0 to 15
- source_position: int32 [3], replicated, may hold values from 0 to 23
- momenta: int32 [27, 3], replicated, may hold values from -3 to 3
- gamma_table: int32 [16], replicated, may hold values from 0 to 15, each once
Outputs:
- correlator: float32 [2, 16, 16, 27], P(None, 'ta', 'gz')
Inputs may be any that keep to these rules, and one draw needn't show every extreme that they name: `gamma_table`: each of 0 to 15 appears exactly once.
All inputs are finite; a program needn't handle non-finite values.
Results may differ from a plain program's by a relative error of at most 0.00007.
Values sent between devices are 32-bit elements; how exact they have to be, the bound alone decides.
A program may use at most 192 MiB of HBM per device.

v0:
```python
import math

import jax
import jax.numpy as jnp
import numpy as np
from jax import lax
from jax.experimental import pallas as pl
from jax.experimental.pallas import tpu as pltpu
from jax.sharding import PartitionSpec as P

L = 24
NG = 16


def gamma_tables():
    paulis = [
        np.eye(2),
        np.array([[0.0, 1.0], [1.0, 0.0]]),
        np.array([[0.0, -1j], [1j, 0.0]]),
        np.array([[1.0, 0.0], [0.0, -1.0]]),
    ]
    matrices = np.stack([np.kron(paulis[number // 4], paulis[number % 4]) for number in range(16)])
    return np.stack([matrices.real, matrices.imag]).astype(np.float32)


def complex_product(einsum_form, left_term, right_term):

    def product(first_op, second_op):
        return jnp.einsum(einsum_form, first_op, second_op, precision=lax.Precision.HIGHEST)

    real_part = product(left_term[0], right_term[0]) - product(left_term[1], right_term[1])
    imag_part = product(left_term[0], right_term[1]) + product(left_term[1], right_term[0])
    return jnp.stack([real_part, imag_part])


LANES = 128
SUBLANES = 8
PAIRS = [(row, column) for row in range(12) for column in range(row, 12)]
PAIR_NUMBER = {pair: number for number, pair in enumerate(PAIRS)}


def multiply_add(total, left, right):
    real = left[0] * right[0] - left[1] * right[1]
    imag = left[0] * right[1] + left[1] * right[0]
    return (real, imag) if total is None else (total[0] + real, total[1] + imag)


def multiply_add_conj(total, left, right):
    real = left[0] * right[0] + left[1] * right[1]
    imag = left[1] * right[0] - left[0] * right[1]
    return (real, imag) if total is None else (total[0] + real, total[1] + imag)


def sink_kernel(owned_ref, s_ref, sigma_ref):
    owned = owned_ref[0] == 1

    @pl.when(owned)
    def _():
        for row in range(12):
            left = [(s_ref[row * 12 + m], s_ref[144 + row * 12 + m]) for m in range(12)]
            for column in range(row, 12):
                total = None
                for m in range(12):
                    right = (s_ref[column * 12 + m], s_ref[144 + column * 12 + m])
                    total = multiply_add(total, left[m], right)
                number = PAIR_NUMBER[row, column]
                sigma_ref[number] = 0.125 * total[0]
                sigma_ref[len(PAIRS) + number] = 0.125 * total[1]

    @pl.when(jnp.logical_not(owned))
    def _():
        sigma_ref[...] = jnp.zeros_like(sigma_ref)


def spin_kernel(s_ref, h_ref, sigma_ref, m_ref):
    def one_spin(alpha, carry):
        sums = [None] * 4
        for color in range(3):
            base = (alpha * 3 + color) * 12
            h_row = [(h_ref[base + m], h_ref[144 + base + m]) for m in range(12)]
            b_row = []
            for k in range(12):
                total = None
                for m in range(12):
                    number = PAIR_NUMBER[min(m, k), max(m, k)]
                    sigma = (sigma_ref[number], sigma_ref[len(PAIRS) + number])
                    total = multiply_add(total, h_row[m], sigma)
                b_row.append(total)
            for beta in range(4):
                start = (beta * 3 + color) * 12
                for m in range(12):
                    forward = (s_ref[start + m], s_ref[144 + start + m])
                    sums[beta] = multiply_add_conj(sums[beta], forward, b_row[m])
        for beta in range(4):
            m_ref[beta * 4 + alpha] = sums[beta][0]
            m_ref[16 + beta * 4 + alpha] = sums[beta][1]
        return carry

    lax.fori_loop(0, 4, one_spin, 0)


def site_block(rows):
    return pl.BlockSpec((rows, SUBLANES, LANES), lambda step: (0, step, 0))


def sink_source(owned, sites):
    rows = sites.shape[1]
    return pl.pallas_call(
        sink_kernel,
        grid=(pl.cdiv(rows, SUBLANES),),
        in_specs=[pl.BlockSpec(memory_space=pltpu.SMEM), site_block(288)],
        out_specs=site_block(2 * len(PAIRS)),
        out_shape=jax.ShapeDtypeStruct((2 * len(PAIRS), rows, LANES), jnp.float32),
        name="sink_source",
    )(owned, sites)


def spin_blocks(forward, back_field, sigma):
    rows = forward.shape[1]
    return pl.pallas_call(
        spin_kernel,
        grid=(pl.cdiv(rows, SUBLANES),),
        in_specs=[site_block(288), site_block(288), site_block(2 * len(PAIRS))],
        out_specs=site_block(32),
        out_shape=jax.ShapeDtypeStruct((32, rows, LANES), jnp.float32),
        name="spin_blocks",
    )(forward, back_field, sigma)


def tiles(field):
    local_times, site_count = field.shape[3:]
    flat = field.reshape(288, local_times, site_count // LANES, LANES)
    return [flat[:, time] for time in range(local_times)]


def phase_table(site_index, source_position, momenta):
    zplane = site_index // (L * L)
    xline = site_index // L % L
    yline = site_index % L
    wave = (
        momenta[:, 0:1] * (xline[None, :] - source_position[0])
        + momenta[:, 1:2] * (yline[None, :] - source_position[1])
        + momenta[:, 2:3] * (zplane[None, :] - source_position[2])
    )
    wave = jnp.mod(wave, L)
    angle_value = wave.astype(jnp.float32) * (2.0 * math.pi / L)
    return jnp.stack([jnp.cos(angle_value), -jnp.sin(angle_value)])


def select_currents(gamma_table, values):
    onehot = (gamma_table[:, None] == jnp.arange(NG, dtype=jnp.int32)[None, :]).astype(jnp.float32)
    return jnp.einsum("cg,xgp->xcp", onehot, values, precision=lax.Precision.HIGHEST)


def body(propagator, backward, sink_time, source_position, momenta, gamma_table):
    gamma_flat = jnp.asarray(np.transpose(gamma_tables(), (0, 1, 3, 2)).reshape(2, 16, 16))
    local_times = propagator.shape[3]
    site_count = propagator.shape[4]
    local_time = sink_time[0] - lax.axis_index("ta") * local_times
    owned = jnp.logical_and(local_time >= 0, local_time < local_times)
    local_index = jnp.clip(local_time, 0, local_times - 1)
    forwards, backwards = tiles(propagator), tiles(backward)
    sink_slice = forwards[0]
    for time in range(1, local_times):
        sink_slice = jnp.where(local_index == time, forwards[time], sink_slice)
    sigma = lax.psum(sink_source(owned.astype(jnp.int32)[None], sink_slice), "ta")
    first_site = lax.axis_index("gz") * site_count
    phases = phase_table(
        first_site + jnp.arange(site_count, dtype=jnp.int32), source_position, momenta
    )
    momentum_count = momenta.shape[0]
    phase_rows = phases.reshape(2 * momentum_count, site_count)
    scale_factor = 1.0 / (72.0 * math.sqrt(L * L * L))
    stacked = []
    for time in range(local_times):
        spin = spin_blocks(forwards[time], backwards[time], sigma)
        sums = jnp.einsum(
            "bs,ps->bp",
            spin.reshape(32, site_count),
            phase_rows,
            precision=lax.Precision.HIGHEST,
        ).reshape(2, 16, 2, momentum_count)
        real = sums[0, :, 0] - sums[1, :, 1]
        imag = sums[0, :, 1] + sums[1, :, 0]
        currents = complex_product("gb,bp->gp", gamma_flat, jnp.stack([real, imag]))
        stacked.append(select_currents(gamma_table, scale_factor * currents))
    local_sums = jnp.stack(stacked, axis=1)
    return lax.psum_scatter(local_sums, "gz", scatter_dimension=2, tiled=True)


def solution(mesh):
    in_specs = (
        P(None, None, None, "ta", "gz"),
        P(None, None, None, "ta", "gz"),
        P(),
        P(),
        P(),
        P(),
    )
    out_specs = P(None, "ta", "gz", None)
    return jax.shard_map(body, mesh=mesh, in_specs=in_specs, out_specs=out_specs, check_vma=False)
```

profile of v0, /device:TPU:0, one launch (start us, length us, event | category | flops | bytes accessed | tf_op | source)
XLA Modules:
  0.0 268.5 jit_solution(9199361619230630060)
XLA Ops:
  6.5 25.1 %reduce = f32[2,12,12,6912]{3,2,1,0:T(8,128)} reduce(f32[2,12,12,1,6912]{4,3,2,1,0:T(1,128)} %param.7, f32[]{:T(128)} %constant.60), dimensions={3}, to_apply=%param.7.reduce_sub_computation | reduce | bytes 15925252 | tf_op args[0]
  31.7 9.7 %squeeze_reshape.6.s_ref = f32[288,54,128]{2,1,0:T(8,128)} reshape(f32[2,12,12,6912]{3,2,1,0:T(8,128)} %reduce) | data formatting | bytes 15925248 | tf_op jit(solution)/shard_map/squeeze;reshape | solution.py:133
  42.0 7.8 %sink_source.1 = f32[156,54,128]{2,1,0:T(8,128)} custom-call(s32[1]{0:T(128)} %bitcast.1.owned_ref, f32[288,54,128]{2,1,0:T(8,128)} %squeeze_reshape.6.s_ref), custom_call_target="tpu_custom_call" | custom-call | tf_op jit(solution)/shard_map/sink_source/pallas_call | solution.py:108
  49.9 0.0 all-reduce.2.cloned.1.call-update
  49.9 0.2 reduce-scatter.2.cloned.1.call-start
  50.1 25.1 %reduce.1 = f32[2,12,12,6912]{3,2,1,0:T(8,128)} reduce(f32[2,12,12,1,6912]{4,3,2,1,0:T(1,128)} %param.8, f32[]{:T(128)} %constant.60), dimensions={3}, to_apply=%param.8.reduce_sub_computation | reduce | bytes 15925252 | tf_op args[1]
  75.2 9.8 %squeeze_reshape.7.h_ref = f32[288,54,128]{2,1,0:T(8,128)} reshape(f32[2,12,12,6912]{3,2,1,0:T(8,128)} %reduce.1) | data formatting | bytes 15925248 | tf_op jit(solution)/shard_map/squeeze;reshape | solution.py:133
  85.1 0.6 fusion.38
  85.7 0.6 fusion.15
  86.3 1.3 fusion.13
  87.7 3.8 %fusion.11 = (f32[1,27,6912]{2,1,0:T(8,128)S(1)}, f32[1,27,6912]{2,1,0:T(8,128)S(1)}) fusion(s32[6912]{0:T(1024)S(1)} %fusion.15, s32[27]{0:T(128)S(1)} %get-tuple-element.8, s32[6912]{0:T(1024)S(1)} %get-tuple-element.14, s32[27]{0:T(128)S(1)} %get-tuple-element.9, s32[6912]{0:T(1024)S(1)} %get-tuple-element.13, s32[27]{0:T(128)S(1)} %get-tuple-element.7), kind=kLoop, calls=%fused_computation.18 | loop fusion | flops 2612736 | bytes 1576260 | tf_op jit(solution)/shard_map/cos | solution.py:147
  91.4 0.0 copy-start
  91.5 0.0 copy-start.1
  91.5 136.4 %all-reduce.2.cloned.1.call-done.sigma_ref = f32[156,54,128]{2,1,0:T(8,128)} async-done(((f32[156,54,128]{2,1,0:T(8,128)}), f32[156,54,128]{2,1,0:T(8,128)}) %all-reduce.2.cloned.1.call-update) | async-done | bytes 4313104 | tf_op jit(solution)/shard_map/psum | solution.py:166
  227.9 20.3 %spin_blocks.1 = f32[32,54,128]{2,1,0:T(8,128)} custom-call(f32[288,54,128]{2,1,0:T(8,128)} %squeeze_reshape.6.s_ref, f32[288,54,128]{2,1,0:T(8,128)} %squeeze_reshape.7.h_ref, f32[156,54,128]{2,1,0:T(8,128)} %all-reduce.2.cloned.1.call-done.sigma_ref), custom_call_target="tpu_custom_call" | custom-call | tf_op jit(solution)/shard_map/spin_blocks/pallas_call | solution.py:120
  248.2 1.3 reshape.393
  249.5 4.1 %fusion = f32[2,16,2,27]{3,1,2,0:T(8,128)S(1)} fusion(f32[1,27,6912]{2,1,0:T(8,128)S(1)} %get-tuple-element.6, f32[1,27,6912]{2,1,0:T(8,128)S(1)} %get-tuple-element.5, f32[2,16,6912,1]{2,1,0,3:T(8,128)S(1)} %reshape.393), kind=kOutput, calls=%fused_computation.1 | convolution fusion | flops 143700480 | bytes 2384640 | tf_op jit(solution)/shard_map/bs,ps->bp/dot_general | solution.py:177
  253.6 0.1 fusion.32
  253.7 0.1 fusion.30
  253.9 0.1 fusion.3
  254.0 0.1 fusion.4
  254.2 0.8 convolution_bitcast_fusion
  255.0 0.0 reduce-scatter.2.cloned.1.call-update
  255.0 6.7 %reduce-scatter.2.cloned.1.call-done = f32[2,1,8,27]{3,2,0,1:T(8,128)} async-done(((f32[2,1,16,27]{3,2,0,1:T(8,128)}), f32[2,1,8,27]{3,2,0,1:T(8,128)}) %reduce-scatter.2.cloned.1.call-update) | async-done | bytes 1744 | tf_op jit(solution)/shard_map/reduce_scatter | solution.py:188
  (10 shorter events, 0.0 us)
Async XLA Ops:
  6.5 221.3 %all-reduce.2.cloned.1.call-start = ((), (), s32[]{:S(2)}) async-start(), calls=%async_computation.1 | async-start | bytes 8945664 | tf_op jit(solution)/shard_map/psum | solution.py:166
  49.9 211.8 %reduce-scatter.2.cloned.1.call-start = ((), (), s32[]{:S(2)}) async-start(), calls=%async_computation.2 | async-start | bytes 24576 | tf_op jit(solution)/shard_map/reduce_scatter | solution.py:188
  75.2 9.8 %copy-start.2 = (s32[3]{0:T(128)S(1)}, s32[3]{0:T(128)}, u32[]{:S(2)}) copy-start(s32[3]{0:T(128)} %param.10) | copy-start | bytes 40
  75.2 12.4 %copy-start.3 = (s32[27,3]{0,1:T(4,128)S(1)}, s32[27,3]{0,1:T(4,128)}, u32[]{:S(2)}) copy-start(s32[27,3]{0,1:T(4,128)} %param.11) | copy-start | bytes 976
  91.4 162.2 %copy-start = (f32[16,16]{1,0:T(8,128)S(1)}, f32[16,16]{1,0:T(8,128)}, u32[]{:S(2)}) copy-start(f32[16,16]{1,0:T(8,128)} %constant.57) | copy-start | bytes 3076
  91.5 162.4 %copy-start.1 = (f32[16,16]{1,0:T(8,128)S(1)}, f32[16,16]{1,0:T(8,128)}, u32[]{:S(2)}) copy-start(f32[16,16]{1,0:T(8,128)} %constant.59) | copy-start | bytes 3076
  91.5 162.7 %copy-start.4 = (s32[16]{0:T(128)S(1)}, s32[16]{0:T(128)}, u32[]{:S(2)}) copy-start(s32[16]{0:T(128)} %param.12) | copy-start | bytes 196
Sparse Core Ops, SparseCore 0:
  50.0 177.8 all-reduce.1
  255.1 6.5 reduce-scatter.1
where the time goes:
time: 269 us
  waiting for transfers between devices  143 us (53%)
  other arithmetic  56 us (21%)
  Pallas kernels  28.1 us (10%)
  local copies, waits for them, and re-layouts  21.5 us (8%)
  between operations  14.2 us (5%)
  matrix products  5.44 us (2%)
    psum x1, waiting for transfers between devices, body(): lax.psum(sink_source(owned.astype(jnp.int32)[None], sink_slice), 'ta')  136 us
    unnamed x2, other arithmetic  50.3 us
    pallas_call x1, Pallas kernels, spin_blocks(): pl.pallas_call(spin_kernel, grid=(pl.cdiv(rows, SUBLANES),), in_specs=[si...  20.3 us
    another operation x2, local copies, waits for them, and re-layouts, tiles(): return [flat[:, time] for time in range(local_times)]  19.5 us
    pallas_call x1, Pallas kernels, sink_source(): pl.pallas_call(sink_kernel, grid=(pl.cdiv(rows, SUBLANES),), in_specs=[pl...  7.82 us
    reduce_scatter x1, waiting for transfers between devices, body(): return lax.psum_scatter(local_sums, 'gz', scatter_dimension=2, tiled=True)  6.68 us
  transfers between devices with their start and end apart: 2, of which 2 were waited for; matrix products, arithmetic and copies ran while one was open for 15% of the time, Pallas kernels for 0%

commit v1 on v0

v1 whole, which is shorter than its diff:
```python
import math
import random

import jax
import jax.numpy as jnp
import numpy as np
from jax import lax
from jax.experimental import pallas as pl
from jax.experimental.pallas import tpu as pltpu
from jax.sharding import PartitionSpec as P

L = 24
NG = 16
LANES = 128
SUB = 8
SPINCOLOR = 12
COMPS = 2 * SPINCOLOR * SPINCOLOR
PAIRS = [(row, column) for row in range(SPINCOLOR) for column in range(row, SPINCOLOR)]
PAIR_NUMBER = {pair: number for number, pair in enumerate(PAIRS)}
HOP_SLOTS = 6
MESH = pl.DeviceIdType.MESH
HIGHEST = lax.Precision.HIGHEST


def gamma_tables():
    paulis = [
        np.eye(2),
        np.array([[0.0, 1.0], [1.0, 0.0]]),
        np.array([[0.0, -1j], [1j, 0.0]]),
        np.array([[1.0, 0.0], [0.0, -1.0]]),
    ]
    matrices = np.stack([np.kron(paulis[number // 4], paulis[number % 4]) for number in range(16)])
    return np.stack([matrices.real, matrices.imag]).astype(np.float32)


class Grid:
    def __init__(self, mesh):
        devices = mesh.devices.reshape(mesh.shape["ta"], -1)[:, 0]
        self.nodes = len(devices)
        self.dims, self.strides, self.wrap = [self.nodes], [1], False
        coords = [getattr(device, "coords", None) for device in devices]
        if all(coord is not None for coord in coords):
            self.read(np.array([list(coord) for coord in coords]))
        self.dirs = []
        for axis, size in enumerate(self.dims):
            if size == 2:
                self.dirs.append((axis, 0))
            elif size > 2:
                self.dirs += [(axis, 1), (axis, -1)]

    def read(self, coords):
        coords = coords - coords.min(axis=0)
        sizes = coords.max(axis=0) + 1
        found = []
        for axis in range(coords.shape[1]):
            if sizes[axis] > 1:
                unit = np.zeros(coords.shape[1], int)
                unit[axis] = 1
                hits = np.flatnonzero((coords == unit).all(axis=1))
                if len(hits) != 1:
                    return
                found.append((int(hits[0]), int(sizes[axis]), axis))
        found.sort(reverse=True)
        index = np.arange(self.nodes)
        for stride, size, axis in found:
            if ((index // stride) % size != coords[:, axis]).any():
                return
        if math.prod(size for _, size, _ in found) != self.nodes:
            return
        self.dims = [size for _, size, _ in found]
        self.strides = [stride for stride, _, _ in found]
        self.wrap = len(found) == 3 and all(size % 4 == 0 for size in self.dims)

    def position(self, node):
        return [node // stride % size for stride, size in zip(self.strides, self.dims)]

    def node(self, position):
        return sum(c * stride for c, stride in zip(position, self.strides))

    def step(self, node, number):
        axis, sign = self.dirs[number]
        place = self.position(node)
        place[axis] = 1 - place[axis] if sign == 0 else place[axis] + sign
        if self.wrap:
            place[axis] %= self.dims[axis]
        if not 0 <= place[axis] < self.dims[axis]:
            return None
        return self.node(place)


def grow(edges, nodes, root, count, rng, deepest):
    used = set()
    depth = [{root: 0} for _ in range(count)]
    parent = [{} for _ in range(count)]
    from_root = [0] * count
    for _ in range(deepest):
        options = [
            (k, u, d, v)
            for k in range(count)
            for u in depth[k]
            for d, v in edges[u]
            if v not in depth[k] and (u, d) not in used
        ]
        rng.shuffle(options)
        ways = {}
        for k, _, _, v in options:
            ways[k, v] = ways.get((k, v), 0) + 1
        options.sort(key=lambda option: ways[option[0], option[3]] + 1.5 * rng.random())
        level = [{} for _ in range(count)]
        taken = [0] * count
        for k, u, d, v in options:
            if v in depth[k] or v in level[k] or (u, d) in used:
                continue
            if u == root:
                if taken[k] or (from_root[k] and rng.random() < 0.7):
                    continue
                taken[k] = 1
                from_root[k] += 1
            level[k][v] = depth[k][u] + 1
            parent[k][v] = (u, d)
            used.add((u, d))
        for k in range(count):
            depth[k].update(level[k])
        if all(len(known) == nodes for known in depth):
            return sorted(max(known.values()) for known in depth)[::-1], parent, depth
    return None


def route(grid, root):
    edges = {
        u: [
            (d, v)
            for d in range(len(grid.dirs))
            for v in [grid.step(u, d)]
            if v is not None and v != u
        ]
        for u in range(grid.nodes)
    }
    rng = random.Random(7)
    most = min(3, min(len(links) for links in edges.values()))
    for count in range(most, 0, -1):
        best = None
        for _ in range(400 if grid.nodes <= 16 else 40):
            found = grow(edges, grid.nodes, root, count, rng, 2 * sum(grid.dims))
            if found and (best is None or found[0] < best[0]):
                best = found
        if best:
            return count, best[1], best[2]
    raise ValueError("no route")


def routes(grid):
    plans = {}
    for root in range(grid.nodes):
        place = grid.position(root)
        if grid.wrap:
            canonical = 0
        else:
            canonical = grid.node([min(c, n - 1 - c) for c, n in zip(place, grid.dims)])
        if canonical not in plans:
            plans[canonical] = route(grid, canonical)
    trees = min(plan[0] for plan in plans.values())
    width = 1 + 2 * trees + len(grid.dirs)
    table = np.full((grid.nodes, grid.nodes, width), -1, np.int32)
    deepest = 0
    for root in range(grid.nodes):
        place = grid.position(root)
        if grid.wrap:
            canonical, flips = 0, [False] * len(place)
        else:
            flips = [c > n - 1 - c for c, n in zip(place, grid.dims)]
            canonical = grid.node([min(c, n - 1 - c) for c, n in zip(place, grid.dims)])

        def image(node):
            there = grid.position(node)
            if grid.wrap:
                return grid.node([(c + o) % n for c, o, n in zip(there, place, grid.dims)])
            return grid.node([n - 1 - c if f else c for c, f, n in zip(there, flips, grid.dims)])

        def turned(d):
            axis, sign = grid.dirs[d]
            return grid.dirs.index((axis, -sign if flips[axis] else sign))

        _, parent, depth = plans[canonical]
        for k in range(trees):
            for v in range(grid.nodes):
                row = table[image(v), root]
                row[0] = v == canonical
                row[1 + trees + k] = depth[k][v]
                deepest = max(deepest, depth[k][v])
                if v != canonical:
                    u, d = parent[k][v]
                    row[1 + k] = turned(d)
                    sender = table[image(u), root]
                    assert sender[1 + 2 * trees + turned(d)] == -1
                    sender[1 + 2 * trees + turned(d)] = k
    return trees, deepest, table


def multiply_add(total, left, right):
    real = left[0] * right[0] - left[1] * right[1]
    imag = left[0] * right[1] + left[1] * right[0]
    return (real, imag) if total is None else (total[0] + real, total[1] + imag)


def multiply_add_conj(total, left, right):
    real = left[0] * right[0] + left[1] * right[1]
    imag = left[1] * right[0] - left[0] * right[1]
    return (real, imag) if total is None else (total[0] + real, total[1] + imag)


def make_kernel(grid, trees, deepest, rows, momentum_count, currents):
    blocks = pl.cdiv(rows, SUB)
    piece = blocks
    share = 2 * len(PAIRS) // trees
    slots = share * blocks // piece
    hop = HOP_SLOTS
    ring = 2 * hop
    directions = len(grid.dirs)
    all_slots = slots + hop * deepest
    sends = all_slots - hop
    half = SPINCOLOR * SPINCOLOR * rows
    span = half + (SPINCOLOR - 1) * rows + SUB
    sigma_units = 6
    spin_units = SPINCOLOR
    piece_rows = piece * SUB
    padded = 32

    def kernel(
        sink_ref, source_ref, gamma_ref, momenta_ref, mix_ref, table_ref, s_hbm, h_hbm,
        out_ref,
        s_ref, h_ref, own_ref, a_ref, tree_ref, in_ref, stage_ref, phase_ref, m_ref, acc_ref, w_ref,
        send_ref, got_ref, plan_ref,
        load_sem, plan_sem, send_sem, recv_sem, pair_sem,
    ):
        me = lax.axis_index("ta")
        core = lax.axis_index("gz")
        partner = 1 - core
        total_rows = COMPS * rows
        load_s = pltpu.make_async_copy(s_hbm, s_ref.at[pl.ds(0, total_rows)], load_sem.at[0])
        load_h = pltpu.make_async_copy(h_hbm, h_ref.at[pl.ds(0, total_rows)], load_sem.at[1])
        load_s.start()
        load_plan = pltpu.make_async_copy(table_ref.at[me], plan_ref, plan_sem)
        load_plan.start()

        neighbours, has_out, has_in = [], [], []
        for axis, sign in grid.dirs:
            stride, size = grid.strides[axis], grid.dims[axis]
            place = me // stride % size
            if sign == 0:
                neighbours.append(me + stride * (1 - 2 * place))
                has_out.append(None)
                has_in.append(None)
            elif grid.wrap:
                neighbours.append(me + stride * ((place + sign + size) % size - place))
                has_out.append(None)
                has_in.append(None)
            else:
                neighbours.append(me + stride * sign)
                has_out.append(place < size - 1 if sign > 0 else place > 0)
                has_in.append(place > 0 if sign > 0 else place < size - 1)

        def when(condition, action):
            if condition is None:
                action()
            else:
                pl.when(condition)(action)

        barrier = pltpu.get_barrier_semaphore()
        pl.semaphore_signal(barrier, 1, device_id={"gz": partner}, device_id_type=MESH)
        for d in range(directions):

            def greet(d=d):
                pl.semaphore_signal(
                    barrier, 1, device_id={"ta": neighbours[d]}, device_id_type=MESH
                )

            when(has_out[d], greet)

        acc_ref[...] = jnp.zeros_like(acc_ref)
        s_ref[pl.ds(total_rows, SUB)] = jnp.zeros((SUB, LANES), jnp.float32)
        h_ref[pl.ds(total_rows, SUB)] = jnp.zeros((SUB, LANES), jnp.float32)
        names = lax.broadcasted_iota(jnp.int32, (1, NG), 1)
        onehot = jnp.concatenate(
            [
                jnp.where(names == jnp.full((1, NG), gamma_ref[core * currents + c]), 1.0, 0.0)
                for c in range(currents)
            ],
            axis=0,
        )
        for part in range(2):
            w_ref[part * currents : (part + 1) * currents] = lax.dot_general(
                onehot,
                mix_ref[part],
                (((1,), (0,)), ((), ())),
                precision=HIGHEST,
                preferred_element_type=jnp.float32,
            )
        momenta = momenta_ref[...].astype(jnp.float32)
        momenta = jnp.concatenate(
            [momenta, jnp.zeros((padded - momentum_count, 3), jnp.float32)], axis=0
        )
        source = [source_ref[i].astype(jnp.float32) for i in range(3)]

        load_plan.wait()
        sink = sink_ref[0]
        width = 1 + 2 * trees + directions

        def pick(candidate, chosen):
            return tuple(
                jnp.where(sink == candidate, plan_ref[0, candidate * width + q], chosen[q])
                for q in range(width)
            )

        plan = lax.fori_loop(0, grid.nodes, pick, (jnp.int32(-1),) * width)
        everywhere = [jnp.full((SUB, LANES), value, jnp.int32) for value in plan]
        is_source = everywhere[0] == 1
        parents = everywhere[1 : 1 + trees]
        depths = everywhere[1 + trees : 1 + 2 * trees]
        loads = everywhere[1 + 2 * trees :]

        def run(unit, start, stop):
            lax.fori_loop(start, stop, lambda u, carry: (unit(u), carry)[1], 0)

        def sigma_unit(unit):
            block, r = unit // sigma_units, unit % sigma_units
            base = block * SUB
            for i in range(SPINCOLOR + 1):
                first = i < SPINCOLOR - r
                row = jnp.where(first, r, SPINCOLOR - 1 - r)
                column = jnp.where(first, r + i, i - 1)
                total = None
                a = s_ref.at[pl.ds(row * (SPINCOLOR * rows) + base, span)]
                b = s_ref.at[pl.ds(column * (SPINCOLOR * rows) + base, span)]
                for m in range(SPINCOLOR):
                    left = (a[pl.ds(m * rows, SUB)], a[pl.ds(half + m * rows, SUB)])
                    right = (b[pl.ds(m * rows, SUB)], b[pl.ds(half + m * rows, SUB)])
                    total = multiply_add(total, left, right)
                number = row * SPINCOLOR - (row * (row - 1)) // 2 + column - row
                tree = number // (share // 2)
                place = (
                    tree * (share * blocks)
                    + block * share
                    + 2 * (number - tree * (share // 2))
                ) * SUB
                place = pl.multiple_of(place, SUB)
                own_ref[pl.ds(place, SUB)] = 0.125 * total[0]
                own_ref[pl.ds(place + SUB, SUB)] = 0.125 * total[1]

        def phase_row(number):
            lane = lax.broadcasted_iota(jnp.int32, (1, LANES), 1)
            site = (core * (rows * LANES) + number * LANES + lane).astype(jnp.float32)
            zplane = jnp.floor((site + 0.5) * (1.0 / (L * L)))
            rest = site - zplane * (L * L)
            xline = jnp.floor((rest + 0.5) * (1.0 / L))
            yline = rest - xline * L
            wave = (
                momenta[:, 0:1] * (xline - source[0])
                + momenta[:, 1:2] * (yline - source[1])
                + momenta[:, 2:3] * (zplane - source[2])
            )
            wave = wave - L * jnp.floor((wave + 0.5) * (1.0 / L)) - L / 2
            x = wave * (math.pi / L)
            y = x * x
            s = x * (1 + y * (-1 / 6 + y * (1 / 120 + y * (-1 / 5040 + y * (1 / 362880 - y / 39916800)))))
            c = 1 + y * (
                -1 / 2
                + y * (1 / 24 + y * (-1 / 720 + y * (1 / 40320 + y * (-1 / 3628800 + y / 479001600))))
            )
            inside = jnp.where(number < rows, 1.0, 0.0)
            block = number // SUB
            lanes = pl.ds(pl.multiple_of(number % SUB * LANES, LANES), LANES)
            phase_ref[block, 0:padded, lanes] = (2.0 * s * s - 1.0) * inside
            phase_ref[block, padded : 2 * padded, lanes] = (2.0 * s * c) * inside

        def spin_unit(unit):
            block, r = unit // spin_units, unit % spin_units
            alpha, color = r // 3, r % 3
            h = h_ref.at[pl.ds(r * (SPINCOLOR * rows) + block * SUB, span)]
            s = s_ref.at[
                pl.ds(color * (SPINCOLOR * rows) + block * SUB, span + 9 * SPINCOLOR * rows)
            ]
            sigma = [
                tree_ref.at[k, pl.ds(pl.multiple_of(block * (share * SUB), SUB), share * SUB)]
                for k in range(trees)
            ]

            def sigma_at(row, column):
                number = PAIR_NUMBER[min(row, column), max(row, column)]
                tree, place = number // (share // 2), number % (share // 2) * 2 * SUB
                return sigma[tree][place : place + SUB], sigma[tree][place + SUB : place + 2 * SUB]

            h_row = [(h[pl.ds(m * rows, SUB)], h[pl.ds(half + m * rows, SUB)]) for m in range(SPINCOLOR)]
            sums = [None] * 4
            for k in range(SPINCOLOR):
                total = None
                for m in range(SPINCOLOR):
                    total = multiply_add(total, h_row[m], sigma_at(m, k))
                for beta in range(4):
                    start = (beta * 3 * SPINCOLOR + k) * rows
                    forward = (s[pl.ds(start, SUB)], s[pl.ds(half + start, SUB)])
                    sums[beta] = multiply_add_conj(sums[beta], forward, total)
            for beta in range(4):
                for part in range(2):
                    place = pl.ds(pl.multiple_of((part * 16 + beta * 4 + alpha) * SUB, SUB), SUB)
                    m_ref[place] = sums[beta][part] + jnp.where(color > 0, m_ref[place], 0.0)

            @pl.when(r == spin_units - 1)
            def _():
                spin = jnp.concatenate(
                    [m_ref[pl.ds(i, 32, stride=SUB), :] for i in range(SUB)], axis=1
                )
                acc_ref[...] += lax.dot_general(
                    spin,
                    phase_ref[block],
                    (((1,), (1,)), ((), ())),
                    precision=HIGHEST,
                    preferred_element_type=jnp.float32,
                )

        def out_copy(d, slot):
            place = slot % ring
            return pltpu.make_async_remote_copy(
                src_ref=stage_ref.at[d, place],
                dst_ref=in_ref.at[d, place],
                send_sem=send_sem.at[d, place],
                recv_sem=recv_sem.at[d, place],
                device_id={"ta": neighbours[d]},
                device_id_type=MESH,
            )

        def settle(chunk):
            for k in range(trees):
                at_depth = [depths[k] == n for n in range(deepest + 1)]
                for i in range(piece):
                    value = None
                    for n in range(deepest + 1):
                        start = ((chunk + hop * n) * piece + i) * SUB
                        found = a_ref[k, pl.ds(pl.multiple_of(start, SUB), SUB)]
                        value = found if value is None else jnp.where(at_depth[n], found, value)
                    start = pl.multiple_of((chunk * piece + i) * SUB, SUB)
                    tree_ref[k, pl.ds(start, SUB)] = value

        def relay(j):
            @pl.when(j >= hop)
            def _():
                for d in range(directions):
                    when(has_in[d], lambda d=d: out_copy(d, j + hop).wait_recv())

            @pl.when(jnp.logical_and(j >= ring, j < sends + ring))
            def _():
                for d in range(directions):
                    when(has_out[d], lambda d=d: out_copy(d, j).wait_send())

            place = j % ring
            from_place = (j + hop) % ring
            mine = jnp.minimum(j, slots - 1) * piece_rows
            for i in range(piece):
                at = slice(i * SUB, (i + 1) * SUB)
                arrived = [in_ref[d, from_place, at] for d in range(directions)]
                values = []
                for k in range(trees):
                    value = arrived[0]
                    for d in range(1, directions):
                        value = jnp.where(parents[k] == d, arrived[d], value)
                    start = pl.multiple_of(k * (share * blocks * SUB) + mine + i * SUB, SUB)
                    value = jnp.where(is_source, own_ref[pl.ds(start, SUB)], value)
                    a_ref[k, pl.ds(pl.multiple_of(j * piece_rows + i * SUB, SUB), SUB)] = value
                    values.append(value)
                for d in range(directions):
                    value = values[0]
                    for k in range(1, trees):
                        value = jnp.where(loads[d] == k, values[k], value)
                    stage_ref[d, place, at] = value

            @pl.when(j >= hop * deepest)
            def _():
                settle(j - hop * deepest)

            @pl.when(j < sends)
            def _():
                for d in range(directions):
                    when(has_out[d], lambda d=d: out_copy(d, j).start())

        load_s.wait()
        load_h.start()
        run(sigma_unit, 0, sigma_units)

        peers = 1
        for known in has_in:
            peers += 1 if known is None else known.astype(jnp.int32)
        pl.semaphore_wait(barrier, peers)

        def sigma_until(j):
            done = sigma_units + (sigma_units * (blocks * (j + 2)) + slots - 1) // slots
            return jnp.where(j < 0, sigma_units, jnp.minimum(done, sigma_units * blocks))

        phase_count = blocks * SUB

        first = hop * deepest + (share - 1) // piece
        spin_total = spin_units * blocks

        def spin_until(j):
            done = (j - first) * spin_total // slots + 1
            return jnp.where(j < first, 0, jnp.minimum(done, spin_total))

        def step(j, carry):
            relay(j)
            run(sigma_unit, sigma_until(j - 1), sigma_until(j))
            run(
                phase_row,
                jnp.minimum(2 * j, phase_count),
                jnp.minimum(2 * j + 2, phase_count),
            )

            @pl.when(j == first)
            def _():
                load_h.wait()

            run(spin_unit, spin_until(j - 1), spin_until(j))
            return carry

        lax.fori_loop(0, all_slots, step, 0)
        run(spin_unit, spin_until(jnp.int32(all_slots - 1)), spin_total)
        for slot in range(all_slots - ring, sends):
            for d in range(directions):
                when(has_out[d], lambda d=d, slot=slot: out_copy(d, slot).wait_send())

        real = acc_ref[0:16, 0:padded] - acc_ref[16:32, padded : 2 * padded]
        imag = acc_ref[0:16, padded : 2 * padded] + acc_ref[16:32, 0:padded]
        send_ref[0:16, 0:padded] = real
        send_ref[16:32, 0:padded] = imag
        swap = pltpu.make_async_remote_copy(
            src_ref=send_ref,
            dst_ref=got_ref,
            send_sem=pair_sem.at[0],
            recv_sem=pair_sem.at[1],
            device_id={"gz": partner},
            device_id_type=MESH,
        )
        swap.start()
        swap.wait()
        both = send_ref[:, 0:padded] + got_ref[:, 0:padded]
        result = lax.dot_general(
            w_ref[...],
            both,
            (((1,), (0,)), ((), ())),
            precision=HIGHEST,
            preferred_element_type=jnp.float32,
        )
        out_ref[0, 0] = result[0:currents, 0:momentum_count]
        out_ref[1, 0] = result[currents : 2 * currents, 0:momentum_count]

    scratch = [
        pltpu.VMEM((COMPS * rows + SUB, LANES), jnp.float32),
        pltpu.VMEM((COMPS * rows + SUB, LANES), jnp.float32),
        pltpu.VMEM((trees * share * blocks * SUB, LANES), jnp.float32),
        pltpu.VMEM((trees, all_slots * piece_rows, LANES), jnp.float32),
        pltpu.VMEM((trees, share * blocks * SUB, LANES), jnp.float32),
        pltpu.VMEM((directions, ring, piece_rows, LANES), jnp.float32),
        pltpu.VMEM((directions, ring, piece_rows, LANES), jnp.float32),
        pltpu.VMEM((blocks, 2 * padded, SUB * LANES), jnp.float32),
        pltpu.VMEM((32 * SUB, LANES), jnp.float32),
        pltpu.VMEM((32, 2 * padded), jnp.float32),
        pltpu.VMEM((2 * currents, 32), jnp.float32),
        pltpu.VMEM((32, LANES), jnp.float32),
        pltpu.VMEM((32, LANES), jnp.float32),
        pltpu.SMEM((1, plan_width(grid, trees)), jnp.int32),
        pltpu.SemaphoreType.DMA((2,)),
        pltpu.SemaphoreType.DMA(()),
        pltpu.SemaphoreType.DMA((directions, ring)),
        pltpu.SemaphoreType.DMA((directions, ring)),
        pltpu.SemaphoreType.DMA((2,)),
    ]
    return kernel, scratch


def plan_width(grid, trees):
    used = grid.nodes * (1 + 2 * trees + len(grid.dirs))
    return pl.cdiv(used, LANES) * LANES


def mixing():
    real, imag = np.transpose(gamma_tables(), (0, 1, 3, 2)).reshape(2, 16, 16)
    scale = 1.0 / (72.0 * math.sqrt(L * L * L))
    return (
        scale
        * np.stack([np.concatenate([real, -imag], axis=1), np.concatenate([imag, real], axis=1)])
    ).astype(np.float32)


def solution(mesh):
    grid = Grid(mesh)
    trees, deepest, table = routes(grid)
    cores = mesh.shape["gz"]
    width = plan_width(grid, trees)
    flat = table.reshape(grid.nodes, -1)
    plans = np.zeros((grid.nodes, 1, width), np.int32)
    plans[:, 0, : flat.shape[1]] = flat
    mix = mixing()

    def body(propagator, backward, sink_time, source_position, momenta, gamma_table):
        local_times, site_count = propagator.shape[3:]
        assert local_times == 1 and cores == 2 and site_count % LANES == 0
        rows = site_count // LANES
        momentum_count = momenta.shape[0]
        currents = gamma_table.shape[0] // cores
        kernel, scratch = make_kernel(grid, trees, deepest, rows, momentum_count, currents)
        vmem, smem = (
            pl.BlockSpec(memory_space=pltpu.VMEM),
            pl.BlockSpec(memory_space=pltpu.SMEM),
        )
        anywhere = pl.BlockSpec(memory_space=pl.ANY)
        return pl.pallas_call(
            kernel,
            out_shape=jax.ShapeDtypeStruct((2, 1, currents, momentum_count), jnp.float32),
            in_specs=[smem, smem, smem, vmem, vmem, anywhere, anywhere, anywhere],
            out_specs=vmem,
            scratch_shapes=scratch,
            compiler_params=pltpu.CompilerParams(
                collective_id=0, has_side_effects=True, vmem_limit_bytes=60 << 20
            ),
            name="three_point",
        )(
            sink_time,
            source_position,
            gamma_table,
            momenta,
            jnp.asarray(mix),
            jnp.asarray(plans),
            propagator.reshape(COMPS * rows, LANES),
            backward.reshape(COMPS * rows, LANES),
        )

    in_specs = (
        P(None, None, None, "ta", "gz"),
        P(None, None, None, "ta", "gz"),
        P(),
        P(),
        P(),
        P(),
    )
    out_specs = P(None, "ta", "gz", None)
    return jax.shard_map(body, mesh=mesh, in_specs=in_specs, out_specs=out_specs, check_vma=False)
```

time: 269 us -> 72.7 us (0.27)
  waiting for transfers between devices: 143 us -> 0 us
  other arithmetic: 56 us -> 0 us
  Pallas kernels: 28.1 us -> 69 us
  local copies, waits for them, and re-layouts: 21.5 us -> 2.66 us
  between operations: 14.2 us -> 0.66 us
  matrix products: 5.44 us -> 0 us
    psum x1 -> x0, waiting for transfers between devices: 136 us -> none  [body(): lax.psum(sink_source(owned.astype(jnp.int32)[None], sink_slice), 'ta')]
    unnamed x2 -> x0, other arithmetic: 50.3 us -> none
    pallas_call x2 -> x1, Pallas kernels: 28.1 us -> 69 us  [body(): pl.pallas_call(kernel, out_shape=jax.ShapeDtypeStruct((2, 1, currents, mo...]
    another operation x2 -> x0, local copies, waits for them, and re-layouts: 19.5 us -> none  [tiles(): return [flat[:, time] for time in range(local_times)]]
    reduce_scatter x1 -> x0, waiting for transfers between devices: 6.68 us -> none  [body(): return lax.psum_scatter(local_sums, 'gz', scatter_dimension=2, tiled=True)]
    dot_general x6 -> x0, matrix products: 5.44 us -> none  [the longest x1 4.09 us: body(): jnp.einsum('bs,ps->bp', spin.reshape(32, site_count), phase_rows, precisi...]
    cos x1 -> x0, other arithmetic: 3.76 us -> none  [phase_table(): return jnp.stack([jnp.cos(angle_value), -jnp.sin(angle_value)])]
  transfers between devices with their start and end apart: 2 -> 0, of which waited for: 2 -> 0; matrix products, arithmetic and copies ran while one was open for 15% -> 0% of each run, Pallas kernels for 0% -> 0%
where the time goes in v1:
time: 72.7 us; the launch traced here: 72.3 us
  Pallas kernels  69 us (95%)
  local copies, waits for them, and re-layouts  2.66 us (4%)
    pallas_call x1, Pallas kernels, body(): pl.pallas_call(kernel, out_shape=jax.ShapeDtypeStruct((2, 1, currents, mo...  69 us
    unnamed x2, local copies, waits for them, and re-layouts  2.66 us

profile of v1, /device:TPU:0, one launch (start us, length us, event | category | flops | bytes accessed | tf_op | source)
XLA Modules:
  0.0 72.3 jit_solution(8058907725925664291)
XLA Ops:
  0.7 1.4 %copy.9.momenta_ref = s32[27,3]{1,0:T(8,128)} copy(s32[27,3]{0,1:T(4,128)} %param.12) | data formatting | bytes 648 | tf_op args[4]
  2.0 69.0 %three_point.1 = f32[2,1,8,27]{3,2,1,0:T(8,128)} custom-call(s32[1]{0:T(128)S(6)} %copy.11.sink_ref, s32[3]{0:T(128)} %source_ref.1, s32[16]{0:T(128)} %gamma_ref.1, s32[27,3]{1,0:T(8,128)} %copy.9.momenta_ref, f32[2,16,32]{2,1,0:T(8,128)} %constant.4.clone.mix_ref, s32[16,1,256]{2,1,0:T(1,128)} %constant.5.clone.table_ref, f32[15552,128]{1,0:T(8,128)} %bitcast.2, ...), custom_call_target="tpu_custom_call" | custom-call | tf_op jit(solution)/shard_map/three_point/pallas_call | solution.py:614
  71.0 1.3 %copy.12 = f32[2,1,8,27]{3,2,1,0:T(8,128)} copy(f32[2,1,8,27]{3,2,1,0:T(8,128)} %three_point.1) | data formatting | bytes 3456

commit v2 on v1

--- a/solution.py
+++ b/solution.py
@@ -14,10 +14,10 @@
 LANES = 128
 SUB = 8
 SPINCOLOR = 12
-COMPS = 2 * SPINCOLOR * SPINCOLOR
 PAIRS = [(row, column) for row in range(SPINCOLOR) for column in range(row, SPINCOLOR)]
 PAIR_NUMBER = {pair: number for number, pair in enumerate(PAIRS)}
-HOP_SLOTS = 6
+HOP_SLOTS = (6, 4)
+PIECE = 7
 MESH = pl.DeviceIdType.MESH
 HIGHEST = lax.Precision.HIGHEST
 
@@ -211,34 +211,38 @@
 
 def make_kernel(grid, trees, deepest, rows, momentum_count, currents):
     blocks = pl.cdiv(rows, SUB)
-    piece = blocks
     share = 2 * len(PAIRS) // trees
+    piece = PIECE if share * blocks % PIECE == 0 else blocks
     slots = share * blocks // piece
-    hop = HOP_SLOTS
-    ring = 2 * hop
+    most_hop = max(HOP_SLOTS)
+    ring = 2 * most_hop
     directions = len(grid.dirs)
-    all_slots = slots + hop * deepest
-    sends = all_slots - hop
-    half = SPINCOLOR * SPINCOLOR * rows
-    span = half + (SPINCOLOR - 1) * rows + SUB
     sigma_units = 6
     spin_units = SPINCOLOR
     piece_rows = piece * SUB
+    all_rows = trees * piece_rows
+    ready = [
+        ((2 * PAIR_NUMBER[k, SPINCOLOR - 1] + 1) // trees + 1) / share for k in range(SPINCOLOR)
+    ]
+    behind = math.ceil(100 * max(spin_units * ready[k] - k for k in range(SPINCOLOR)))
     padded = 32
 
     def kernel(
         sink_ref, source_ref, gamma_ref, momenta_ref, mix_ref, table_ref, s_hbm, h_hbm,
         out_ref,
-        s_ref, h_ref, own_ref, a_ref, tree_ref, in_ref, stage_ref, phase_ref, m_ref, acc_ref, w_ref,
-        send_ref, got_ref, plan_ref,
+        s_ref, h_ref, hs_ref, own_ref, a_ref, tree_ref, in_ref, stage_ref, phase_ref,
+        m_ref, acc_ref, w_ref, send_ref, got_ref, plan_ref,
         load_sem, plan_sem, send_sem, recv_sem, pair_sem,
     ):
         me = lax.axis_index("ta")
         core = lax.axis_index("gz")
         partner = 1 - core
-        total_rows = COMPS * rows
-        load_s = pltpu.make_async_copy(s_hbm, s_ref.at[pl.ds(0, total_rows)], load_sem.at[0])
-        load_h = pltpu.make_async_copy(h_hbm, h_ref.at[pl.ds(0, total_rows)], load_sem.at[1])
+        hop = jnp.where(core == 1, HOP_SLOTS[1], HOP_SLOTS[0])
+        all_slots = slots + hop * deepest
+        sends = all_slots - hop
+        inside = pl.ds(0, rows * LANES)
+        load_s = pltpu.make_async_copy(s_hbm, s_ref.at[:, :, :, :, inside], load_sem.at[0])
+        load_h = pltpu.make_async_copy(h_hbm, h_ref.at[:, :, :, :, inside], load_sem.at[1])
         load_s.start()
         load_plan = pltpu.make_async_copy(table_ref.at[me], plan_ref, plan_sem)
         load_plan.start()
@@ -278,8 +282,14 @@
             when(has_out[d], greet)
 
         acc_ref[...] = jnp.zeros_like(acc_ref)
-        s_ref[pl.ds(total_rows, SUB)] = jnp.zeros((SUB, LANES), jnp.float32)
-        h_ref[pl.ds(total_rows, SUB)] = jnp.zeros((SUB, LANES), jnp.float32)
+        spare = (blocks * SUB - rows) * LANES
+        if spare:
+            for field in (s_ref, h_ref):
+                for part in range(2):
+                    for row in range(SPINCOLOR):
+                        field[part, row, :, :, pl.ds(rows * LANES, spare)] = jnp.zeros(
+                            (SPINCOLOR, 1, spare), jnp.float32
+                        )
         names = lax.broadcasted_iota(jnp.int32, (1, NG), 1)
         onehot = jnp.concatenate(
             [
@@ -296,9 +306,18 @@
                 precision=HIGHEST,
                 preferred_element_type=jnp.float32,
             )
-        momenta = momenta_ref[...].astype(jnp.float32)
-        momenta = jnp.concatenate(
-            [momenta, jnp.zeros((padded - momentum_count, 3), jnp.float32)], axis=0
+        eye = jnp.where(
+            lax.broadcasted_iota(jnp.int32, (padded, momentum_count), 0)
+            == lax.broadcasted_iota(jnp.int32, (padded, momentum_count), 1),
+            1.0,
+            0.0,
+        )
+        momenta = lax.dot_general(
+            eye,
+            momenta_ref[...].astype(jnp.float32),
+            (((1,), (1,)), ((), ())),
+            precision=HIGHEST,
+            preferred_element_type=jnp.float32,
         )
         source = [source_ref[i].astype(jnp.float32) for i in range(3)]
 
@@ -322,30 +341,38 @@
         def run(unit, start, stop):
             lax.fori_loop(start, stop, lambda u, carry: (unit(u), carry)[1], 0)
 
+        def take(field, part, row, column, block):
+            sites = pl.ds(pl.multiple_of(block * (SUB * LANES), SUB * LANES), SUB * LANES)
+            return field[part, row, column, :, sites].reshape(SUB, LANES)
+
+        def first_pair(row):
+            return row * SPINCOLOR - lax.div(row * (row - 1), 2)
+
         def sigma_unit(unit):
-            block, r = unit // sigma_units, unit % sigma_units
-            base = block * SUB
+            block, r = lax.div(unit, sigma_units), lax.rem(unit, sigma_units)
+            last = SPINCOLOR - 1 - r
+            upper, lower = first_pair(r) + block * len(PAIRS), first_pair(last) + block * len(PAIRS)
             for i in range(SPINCOLOR + 1):
                 first = i < SPINCOLOR - r
-                row = jnp.where(first, r, SPINCOLOR - 1 - r)
+                row = jnp.where(first, r, last)
                 column = jnp.where(first, r + i, i - 1)
                 total = None
-                a = s_ref.at[pl.ds(row * (SPINCOLOR * rows) + base, span)]
-                b = s_ref.at[pl.ds(column * (SPINCOLOR * rows) + base, span)]
                 for m in range(SPINCOLOR):
-                    left = (a[pl.ds(m * rows, SUB)], a[pl.ds(half + m * rows, SUB)])
-                    right = (b[pl.ds(m * rows, SUB)], b[pl.ds(half + m * rows, SUB)])
+                    left = [take(s_ref, part, row, m, block) for part in range(2)]
+                    right = [take(s_ref, part, column, m, block) for part in range(2)]
                     total = multiply_add(total, left, right)
-                number = row * SPINCOLOR - (row * (row - 1)) // 2 + column - row
-                tree = number // (share // 2)
-                place = (
-                    tree * (share * blocks)
-                    + block * share
-                    + 2 * (number - tree * (share // 2))
-                ) * SUB
-                place = pl.multiple_of(place, SUB)
+                number = jnp.where(first, upper + i, lower + i - 1 - last)
+                place = pl.multiple_of(number * (2 * SUB), SUB)
                 own_ref[pl.ds(place, SUB)] = 0.125 * total[0]
                 own_ref[pl.ds(place + SUB, SUB)] = 0.125 * total[1]
+
+        def sum_unit(unit):
+            row, column = lax.div(unit, SPINCOLOR), lax.rem(unit, SPINCOLOR)
+            for i in range(blocks):
+                start = pl.multiple_of((unit * blocks + i) * SUB, SUB)
+                hs_ref[pl.ds(start, SUB)] = take(h_ref, 0, row, column, i) + take(
+                    h_ref, 1, row, column, i
+                )
 
         def phase_row(number):
             lane = lax.broadcasted_iota(jnp.int32, (1, LANES), 1)
@@ -368,44 +395,47 @@
                 + y * (1 / 24 + y * (-1 / 720 + y * (1 / 40320 + y * (-1 / 3628800 + y / 479001600))))
             )
             inside = jnp.where(number < rows, 1.0, 0.0)
-            block = number // SUB
-            lanes = pl.ds(pl.multiple_of(number % SUB * LANES, LANES), LANES)
+            block = lax.div(number, SUB)
+            lanes = pl.ds(pl.multiple_of(lax.rem(number, SUB) * LANES, LANES), LANES)
             phase_ref[block, 0:padded, lanes] = (2.0 * s * s - 1.0) * inside
             phase_ref[block, padded : 2 * padded, lanes] = (2.0 * s * c) * inside
 
         def spin_unit(unit):
-            block, r = unit // spin_units, unit % spin_units
-            alpha, color = r // 3, r % 3
-            h = h_ref.at[pl.ds(r * (SPINCOLOR * rows) + block * SUB, span)]
-            s = s_ref.at[
-                pl.ds(color * (SPINCOLOR * rows) + block * SUB, span + 9 * SPINCOLOR * rows)
-            ]
-            sigma = [
-                tree_ref.at[k, pl.ds(pl.multiple_of(block * (share * SUB), SUB), share * SUB)]
-                for k in range(trees)
-            ]
-
-            def sigma_at(row, column):
-                number = PAIR_NUMBER[min(row, column), max(row, column)]
-                tree, place = number // (share // 2), number % (share // 2) * 2 * SUB
-                return sigma[tree][place : place + SUB], sigma[tree][place + SUB : place + 2 * SUB]
-
-            h_row = [(h[pl.ds(m * rows, SUB)], h[pl.ds(half + m * rows, SUB)]) for m in range(SPINCOLOR)]
-            sums = [None] * 4
-            for k in range(SPINCOLOR):
-                total = None
-                for m in range(SPINCOLOR):
-                    total = multiply_add(total, h_row[m], sigma_at(m, k))
+            block, k = lax.div(unit, spin_units), lax.rem(unit, spin_units)
+            own_row = first_pair(k) - k
+            column = []
+            for m in range(SPINCOLOR):
+                number = jnp.where(k >= m, PAIR_NUMBER[m, m] - m + k, own_row + m)
+                place = pl.multiple_of((block * len(PAIRS) + number) * (2 * SUB), SUB)
+                real, imag = tree_ref[pl.ds(place, SUB)], tree_ref[pl.ds(place + SUB, SUB)]
+                column.append((real, imag - real, imag + real))
+            for alpha in range(4):
+                sums = [None] * 4
+                for color in range(3):
+                    parts = [None] * 3
+                    for m in range(SPINCOLOR):
+                        row = alpha * 3 + color
+                        start = pl.multiple_of(
+                            ((row * SPINCOLOR + m) * blocks + block) * SUB, SUB
+                        )
+                        back = (
+                            hs_ref[pl.ds(start, SUB)],
+                            take(h_ref, 0, row, m, block),
+                            take(h_ref, 1, row, m, block),
+                        )
+                        for n in range(3):
+                            term = back[n] * column[m][n]
+                            parts[n] = term if parts[n] is None else parts[n] + term
+                    total = (parts[0] - parts[2], parts[0] + parts[1])
+                    for beta in range(4):
+                        forward = [take(s_ref, part, beta * 3 + color, k, block) for part in range(2)]
+                        sums[beta] = multiply_add_conj(sums[beta], forward, total)
                 for beta in range(4):
-                    start = (beta * 3 * SPINCOLOR + k) * rows
-                    forward = (s[pl.ds(start, SUB)], s[pl.ds(half + start, SUB)])
-                    sums[beta] = multiply_add_conj(sums[beta], forward, total)
-            for beta in range(4):
-                for part in range(2):
-                    place = pl.ds(pl.multiple_of((part * 16 + beta * 4 + alpha) * SUB, SUB), SUB)
-                    m_ref[place] = sums[beta][part] + jnp.where(color > 0, m_ref[place], 0.0)
-
-            @pl.when(r == spin_units - 1)
+                    for part in range(2):
+                        place = pl.ds((part * 16 + beta * 4 + alpha) * SUB, SUB)
+                        m_ref[place] = sums[beta][part] + jnp.where(k > 0, m_ref[place], 0.0)
+
+            @pl.when(k == spin_units - 1)
             def _():
                 spin = jnp.concatenate(
                     [m_ref[pl.ds(i, 32, stride=SUB), :] for i in range(SUB)], axis=1
@@ -419,7 +449,7 @@
                 )
 
         def out_copy(d, slot):
-            place = slot % ring
+            place = lax.rem(slot, ring)
             return pltpu.make_async_remote_copy(
                 src_ref=stage_ref.at[d, place],
                 dst_ref=in_ref.at[d, place],
@@ -435,26 +465,26 @@
                 for i in range(piece):
                     value = None
                     for n in range(deepest + 1):
-                        start = ((chunk + hop * n) * piece + i) * SUB
-                        found = a_ref[k, pl.ds(pl.multiple_of(start, SUB), SUB)]
+                        start = (chunk + hop * n) * all_rows + (i * trees + k) * SUB
+                        found = a_ref[pl.ds(pl.multiple_of(start, SUB), SUB)]
                         value = found if value is None else jnp.where(at_depth[n], found, value)
-                    start = pl.multiple_of((chunk * piece + i) * SUB, SUB)
-                    tree_ref[k, pl.ds(start, SUB)] = value
+                    start = chunk * all_rows + (i * trees + k) * SUB
+                    tree_ref[pl.ds(pl.multiple_of(start, SUB), SUB)] = value
 
         def relay(j):
             @pl.when(j >= hop)
             def _():
                 for d in range(directions):
-                    when(has_in[d], lambda d=d: out_copy(d, j + hop).wait_recv())
+                    when(has_in[d], lambda d=d: out_copy(d, j + ring - hop).wait_recv())
 
             @pl.when(jnp.logical_and(j >= ring, j < sends + ring))
             def _():
                 for d in range(directions):
                     when(has_out[d], lambda d=d: out_copy(d, j).wait_send())
 
-            place = j % ring
-            from_place = (j + hop) % ring
-            mine = jnp.minimum(j, slots - 1) * piece_rows
+            place = lax.rem(j, ring)
+            from_place = lax.rem(j + ring - hop, ring)
+            mine = jnp.minimum(j, slots - 1) * all_rows
             for i in range(piece):
                 at = slice(i * SUB, (i + 1) * SUB)
                 arrived = [in_ref[d, from_place, at] for d in range(directions)]
@@ -463,9 +493,10 @@
                     value = arrived[0]
                     for d in range(1, directions):
                         value = jnp.where(parents[k] == d, arrived[d], value)
-                    start = pl.multiple_of(k * (share * blocks * SUB) + mine + i * SUB, SUB)
+                    offset = (i * trees + k) * SUB
+                    start = pl.multiple_of(mine + offset, SUB)
                     value = jnp.where(is_source, own_ref[pl.ds(start, SUB)], value)
-                    a_ref[k, pl.ds(pl.multiple_of(j * piece_rows + i * SUB, SUB), SUB)] = value
+                    a_ref[pl.ds(pl.multiple_of(j * all_rows + offset, SUB), SUB)] = value
                     values.append(value)
                 for d in range(directions):
                     value = values[0]
@@ -492,17 +523,24 @@
         pl.semaphore_wait(barrier, peers)
 
         def sigma_until(j):
-            done = sigma_units + (sigma_units * (blocks * (j + 2)) + slots - 1) // slots
+            done = sigma_units + (3 * sigma_units * (piece * (j + 2)) + 2 * share - 1) // (2 * share)
             return jnp.where(j < 0, sigma_units, jnp.minimum(done, sigma_units * blocks))
 
         phase_count = blocks * SUB
 
-        first = hop * deepest + (share - 1) // piece
+        sum_first, sum_last = 8, hop * deepest - 1
+        sum_total = SPINCOLOR * SPINCOLOR
+
+        def sum_until(j):
+            done = lax.div((j + 1 - sum_first) * sum_total, sum_last - sum_first)
+            return jnp.where(j < sum_first, 0, jnp.minimum(done, sum_total))
+
         spin_total = spin_units * blocks
 
         def spin_until(j):
-            done = (j - first) * spin_total // slots + 1
-            return jnp.where(j < first, 0, jnp.minimum(done, spin_total))
+            there = j - hop * deepest + 1
+            done = (there * (100 * spin_units * piece) // share + 100 - behind) // 100
+            return jnp.where(there <= 0, 0, jnp.clip(done, 0, spin_total))
 
         def step(j, carry):
             relay(j)
@@ -513,18 +551,22 @@
                 jnp.minimum(2 * j + 2, phase_count),
             )
 
-            @pl.when(j == first)
+            @pl.when(j == sum_first)
             def _():
                 load_h.wait()
 
+            run(sum_unit, sum_until(j - 1), sum_until(j))
             run(spin_unit, spin_until(j - 1), spin_until(j))
             return carry
 
         lax.fori_loop(0, all_slots, step, 0)
-        run(spin_unit, spin_until(jnp.int32(all_slots - 1)), spin_total)
-        for slot in range(all_slots - ring, sends):
+        run(spin_unit, spin_until(all_slots - 1), spin_total)
+
+        def sent(slot):
             for d in range(directions):
-                when(has_out[d], lambda d=d, slot=slot: out_copy(d, slot).wait_send())
+                when(has_out[d], lambda d=d: out_copy(d, slot).wait_send())
+
+        run(sent, all_slots - ring, sends)
 
         real = acc_ref[0:16, 0:padded] - acc_ref[16:32, padded : 2 * padded]
         imag = acc_ref[0:16, padded : 2 * padded] + acc_ref[16:32, 0:padded]
@@ -552,11 +594,12 @@
         out_ref[1, 0] = result[currents : 2 * currents, 0:momentum_count]
 
     scratch = [
-        pltpu.VMEM((COMPS * rows + SUB, LANES), jnp.float32),
-        pltpu.VMEM((COMPS * rows + SUB, LANES), jnp.float32),
-        pltpu.VMEM((trees * share * blocks * SUB, LANES), jnp.float32),
-        pltpu.VMEM((trees, all_slots * piece_rows, LANES), jnp.float32),
-        pltpu.VMEM((trees, share * blocks * SUB, LANES), jnp.float32),
+        pltpu.VMEM((2, SPINCOLOR, SPINCOLOR, 1, blocks * SUB * LANES), jnp.float32),
+        pltpu.VMEM((2, SPINCOLOR, SPINCOLOR, 1, blocks * SUB * LANES), jnp.float32),
+        pltpu.VMEM((SPINCOLOR * SPINCOLOR * blocks * SUB, LANES), jnp.float32),
+        pltpu.VMEM((slots * all_rows, LANES), jnp.float32),
+        pltpu.VMEM(((slots + most_hop * deepest) * all_rows, LANES), jnp.float32),
+        pltpu.VMEM((slots * all_rows, LANES), jnp.float32),
         pltpu.VMEM((directions, ring, piece_rows, LANES), jnp.float32),
         pltpu.VMEM((directions, ring, piece_rows, LANES), jnp.float32),
         pltpu.VMEM((blocks, 2 * padded, SUB * LANES), jnp.float32),
@@ -625,11 +668,11 @@
             sink_time,
             source_position,
             gamma_table,
-            momenta,
+            momenta.T,
             jnp.asarray(mix),
             jnp.asarray(plans),
-            propagator.reshape(COMPS * rows, LANES),
-            backward.reshape(COMPS * rows, LANES),
+            propagator,
+            backward,
         )
 
     in_specs = (

time: 72.7 us -> 71.1 us (0.978)
  local copies, waits for them, and re-layouts: 2.66 us -> 1.3 us
    unnamed x2 -> x1, local copies, waits for them, and re-layouts: 2.66 us -> 1.3 us
where the time goes in v2:
time: 71.1 us; the launch traced here: 70.7 us
  Pallas kernels  68.8 us (97%)
  local copies, waits for them, and re-layouts  1.3 us (2%)
    pallas_call x1, Pallas kernels, body(): pl.pallas_call(kernel, out_shape=jax.ShapeDtypeStruct((2, 1, currents, mo...  68.8 us

profile of v2, /device:TPU:0, one launch (start us, length us, event | category | flops | bytes accessed | tf_op | source)
XLA Modules:
  0.0 70.7 jit_solution(1137038752163293727)
XLA Ops:
  0.7 68.8 %three_point.1 = f32[2,1,8,27]{3,2,1,0:T(8,128)} custom-call(s32[1]{0:T(128)S(6)} %copy.10.sink_ref, s32[3]{0:T(128)} %source_ref.1, s32[16]{0:T(128)} %gamma_ref.1, s32[3,27]{1,0:T(4,128)} %bitcast.1, f32[2,16,32]{2,1,0:T(8,128)} %constant.4.clone.mix_ref, s32[16,1,256]{2,1,0:T(1,128)} %constant.5.clone.table_ref, f32[2,12,12,1,6912]{4,3,2,1,0:T(1,128)} %s_hbm.1, ...), custom_call_target="tpu_custom_call" | custom-call | tf_op jit(solution)/shard_map/three_point/pallas_call | solution.py:657
  69.4 1.3 %copy.11 = f32[2,1,8,27]{3,2,1,0:T(8,128)} copy(f32[2,1,8,27]{3,2,1,0:T(8,128)} %three_point.1) | data formatting | bytes 3456

commit v3 on v2

--- a/solution.py
+++ b/solution.py
@@ -16,7 +16,7 @@
 SPINCOLOR = 12
 PAIRS = [(row, column) for row in range(SPINCOLOR) for column in range(row, SPINCOLOR)]
 PAIR_NUMBER = {pair: number for number, pair in enumerate(PAIRS)}
-HOP_SLOTS = (6, 4)
+HOP_SLOTS = (5, 4)
 PIECE = 7
 MESH = pl.DeviceIdType.MESH
 HIGHEST = lax.Precision.HIGHEST

time: 71.1 us -> 71.4 us (level)
  no operation moved by 1% of the time
where the time goes in v3:
time: 71.4 us; the launch traced here: 71.1 us
  Pallas kernels  69.2 us (97%)
  local copies, waits for them, and re-layouts  1.3 us (2%)
    pallas_call x1, Pallas kernels, body(): pl.pallas_call(kernel, out_shape=jax.ShapeDtypeStruct((2, 1, currents, mo...  69.2 us

profile of v3, /device:TPU:0, one launch (start us, length us, event | category | flops | bytes accessed | tf_op | source)
XLA Modules:
  0.0 71.1 jit_solution(6404921882883435272)
XLA Ops:
  0.7 69.2 %three_point.1 = f32[2,1,8,27]{3,2,1,0:T(8,128)} custom-call(s32[1]{0:T(128)S(6)} %copy.10.sink_ref, s32[3]{0:T(128)} %source_ref.1, s32[16]{0:T(128)} %gamma_ref.1, s32[3,27]{1,0:T(4,128)} %bitcast.1, f32[2,16,32]{2,1,0:T(8,128)} %constant.4.clone.mix_ref, s32[16,1,256]{2,1,0:T(1,128)} %constant.5.clone.table_ref, f32[2,12,12,1,6912]{4,3,2,1,0:T(1,128)} %s_hbm.1, ...), custom_call_target="tpu_custom_call" | custom-call | tf_op jit(solution)/shard_map/three_point/pallas_call | solution.py:657
  69.8 1.3 %copy.11 = f32[2,1,8,27]{3,2,1,0:T(8,128)} copy(f32[2,1,8,27]{3,2,1,0:T(8,128)} %three_point.1) | data formatting | bytes 3456
